TPU v7x, 32 devices: a whole 2x2x4 slice. The times are simulated.
32 devices in a mesh: rows: 8 (over z, x), cols: 4 (over y, core).
Axes of the slice: x: 2, y: 2, z: 4, core: 2. Of those that a mesh axis runs over, the one named last changes fastest.
Arguments:
- tables: float32 [4, 4096, 512], P(None, 'rows', 'cols'), may hold values from -1.5 to 1.5
- dense_features: float32 [256, 512], P('rows', 'cols'), may hold values from -6 to 6
- slot_rows: int32 [8, 8, 4, 64], P('rows'), may hold values from 0 to 511, as said below
- slot_examples: int32 [8, 8, 4, 64], P('rows'), may hold values from 0 to 31, as said below
- slot_counts: int32 [8, 8, 4], P('rows'), may hold values from 21 to 64, as said below
Outputs:
- pooled: float32 [256, 4, 512], P('rows', None, 'cols')
- interactions: float32 [256, 10], P('rows')
Inputs may be any that keep to these rules, and one draw needn't show every extreme that they name: slot_rows[s, o, t, c] names row o * 512 + value of table t. `slot_examples`: an example of the source device s. `slot_counts`: slots 0 to count - 1 of a bucket are live, the others unused; some bucket of every draw is full.
All inputs are finite; a program needn't handle non-finite values.
Results may differ from a plain program's by a relative error of at most 0.0003.
Values sent between devices are 32-bit elements; how exact they have to be, the bound alone decides.
A program may use at most 64 MiB of HBM per device.

v0:
```python
import jax
import jax.numpy as jnp
from jax import lax
from jax.sharding import PartitionSpec as P

E = 512


def lookup(got_rows, tables):
    range_rows = tables.shape[1]
    row_ids = jnp.arange(range_rows, dtype=jnp.int32)

    def one_table(pieces):
        rows_table, table_slice = pieces
        selector = (rows_table[:, :, None] == row_ids[None, None, :]).astype(jnp.float32)
        return jnp.einsum("scr,re->sce", selector, table_slice, precision=lax.Precision.HIGHEST)

    picked = lax.map(one_table, (jnp.moveaxis(got_rows, 1, 0), tables))
    return jnp.moveaxis(picked, 0, 1)


def upper_pairs(gram_matrix, count):
    pieces = [gram_matrix[:, first, first + 1 :] for first in range(count - 1)]
    return jnp.concatenate(pieces, axis=1)


def body(tables, dense_features, slot_rows, slot_examples, slot_counts):
    table_count = tables.shape[0]
    capacity = slot_rows.shape[3]
    examples_here = dense_features.shape[0]
    slot_index = jnp.arange(capacity, dtype=jnp.int32)
    example_ids = jnp.arange(examples_here, dtype=jnp.int32)
    got_rows = lax.all_to_all(slot_rows, "rows", split_axis=1, concat_axis=0, tiled=True)
    looked = lookup(got_rows[:, 0], tables)
    returned = lax.all_to_all(looked[:, None], "rows", split_axis=0, concat_axis=1, tiled=True)
    source_live = slot_index[None, None, :] < slot_counts[0][:, :, None]
    onehot = (
        (slot_examples[0][:, :, :, None] == example_ids[None, None, None, :])
        & source_live[:, :, :, None]
    ).astype(jnp.float32)
    pooled = jnp.einsum("otcb,otce->bte", onehot, returned[0], precision=lax.Precision.HIGHEST)
    vectors = jnp.concatenate([dense_features[:, None, :], pooled], axis=1)
    complete = lax.all_gather(vectors, "cols", axis=2, tiled=True)
    gram_matrix = jnp.einsum("bie,bje->bij", complete, complete, precision=lax.Precision.HIGHEST)
    interactions = upper_pairs(gram_matrix, table_count + 1) * E ** (-0.5)
    return (pooled, interactions)


def solution(mesh):
    placed = (
        P(None, "rows", "cols"),
        P("rows", "cols"),
        P("rows", None, None, None),
        P("rows", None, None, None),
        P("rows", None, None),
    )
    return jax.shard_map(
        body,
        mesh=mesh,
        in_specs=placed,
        out_specs=(P("rows", None, "cols"), P("rows", None)),
        check_vma=False,
    )
```

profile of v0, /device:TPU:0, one launch (start us, length us, event | category | flops | bytes accessed | tf_op | source)
XLA Modules:
  0.0 65.1 jit_solution(7228471273788567425)
XLA Ops:
  0.6 0.0 copy-start
  0.6 0.7 %copy-done = s32[1,8,4,64]{3,2,1,0:T(4,128)S(1)} copy-done((s32[1,8,4,64]{3,2,1,0:T(4,128)S(1)}, s32[1,8,4,64]{3,2,1,0:T(4,128)}, u32[]{:S(2)}) %copy-start) | copy-done | bytes 8216
  1.4 0.7 %reshape.23 = s32[8,1,256]{2,1,0:T(1,128)} reshape(s32[8,1,4,64]{3,2,1,0:T(4,128)S(1)} %bitcast_bitcast_fusion.1) | data formatting | bytes 16384
  2.0 7.3 %all-to-all-start = ((s32[8,1,256]{2,1,0:T(1,128)}), s32[8,1,256]{2,1,0:T(1,128)S(1)}, u32[]{:S(2)}, u32[]{:S(2)}) async-start(s32[8,1,256]{2,1,0:T(1,128)} %reshape.23), calls=%async_computation | async-start | bytes 16384 | tf_op jit(solution)/shard_map/all_to_all | solution.py:33
  9.3 6.5 %all-to-all-done = s32[8,1,256]{2,1,0:T(1,128)S(1)} async-done(((s32[8,1,256]{2,1,0:T(1,128)}), s32[8,1,256]{2,1,0:T(1,128)S(1)}, u32[]{:S(2)}, u32[]{:S(2)}) %all-to-all-start) | async-done | bytes 8224 | tf_op jit(solution)/shard_map/all_to_all | solution.py:33
  15.8 0.5 broadcast.7
  16.4 0.7 %reduce.2 = s32[8,256]{1,0:T(8,128)S(1)} reduce(s32[8,1,256]{2,1,0:T(1,128)S(1)} %all-to-all-done, s32[]{:T(128)} %broadcast.7), dimensions={1}, to_apply=%all_to_all.4.reduce_sub_computation | reduce | bytes 16388 | tf_op jit(solution)/shard_map/all_to_all | solution.py:33
  17.0 0.1 reshape.24
  17.1 9.2 %while.11 = (s32[]{:T(128)}, f32[4,8,64,128]{3,2,0,1:T(8,128)}, s32[4,8,64]{2,0,1:T(4,128)S(1)}, f32[4,512,128]{2,1,0:T(8,128)}, s32[]{:T(128)}) while((s32[]{:T(128)}, f32[4,8,64,128]{3,2,0,1:T(8,128)}, s32[4,8,64]{2,0,1:T(4,128)S(1)}, f32[4,512,128]{2,1,0:T(8,128)}, s32[]{:T(128)}) %tuple.29), condition=%wide.region_1.2_spmd.clone, body=%wide.region_0.1_spmd.clone.sunk | while | flops 402915328 | bytes 531521 | solution.py:18
  17.1 2.3 %fusion.18 = f32[4,8,64,128]{3,2,0,1:T(8,128)} fusion(f32[4,8,64,128]{3,2,0,1:T(8,128)} %get-tuple-element.89, s32[]{:T(128)} %get-tuple-element.88, s32[8,64]{1,0:T(8,128)S(1)} %bitcast.47, f32[4,512,128]{2,1,0:T(8,128)} %get-tuple-element.96), kind=kOutput, calls=%fused_computation.2.clone.1 | convolution fusion | flops 402915328 | bytes 527360 | tf_op jit(solution)/shard_map/while/body/eval_jaxpr/scr,re->sce/dot_general | solution.py:16
  19.5 2.3 %fusion.18 = f32[4,8,64,128]{3,2,0,1:T(8,128)} fusion(f32[4,8,64,128]{3,2,0,1:T(8,128)} %get-tuple-element.89, s32[]{:T(128)} %get-tuple-element.88, s32[8,64]{1,0:T(8,128)S(1)} %bitcast.47, f32[4,512,128]{2,1,0:T(8,128)} %get-tuple-element.96), kind=kOutput, calls=%fused_computation.2.clone.1 | convolution fusion | flops 402915328 | bytes 527360 | tf_op jit(solution)/shard_map/while/body/eval_jaxpr/scr,re->sce/dot_general | solution.py:16
  21.8 2.3 %fusion.18 = f32[4,8,64,128]{3,2,0,1:T(8,128)} fusion(f32[4,8,64,128]{3,2,0,1:T(8,128)} %get-tuple-element.89, s32[]{:T(128)} %get-tuple-element.88, s32[8,64]{1,0:T(8,128)S(1)} %bitcast.47, f32[4,512,128]{2,1,0:T(8,128)} %get-tuple-element.96), kind=kOutput, calls=%fused_computation.2.clone.1 | convolution fusion | flops 402915328 | bytes 527360 | tf_op jit(solution)/shard_map/while/body/eval_jaxpr/scr,re->sce/dot_general | solution.py:16
  24.1 2.3 %fusion.18 = f32[4,8,64,128]{3,2,0,1:T(8,128)} fusion(f32[4,8,64,128]{3,2,0,1:T(8,128)} %get-tuple-element.89, s32[]{:T(128)} %get-tuple-element.88, s32[8,64]{1,0:T(8,128)S(1)} %bitcast.47, f32[4,512,128]{2,1,0:T(8,128)} %get-tuple-element.96), kind=kOutput, calls=%fused_computation.2.clone.1 | convolution fusion | flops 402915328 | bytes 527360 | tf_op jit(solution)/shard_map/while/body/eval_jaxpr/scr,re->sce/dot_general | solution.py:16
  26.3 0.0 copy-start.2
  26.3 0.0 copy-start.3
  26.3 3.7 %all-to-all-start.1 = ((f32[8,1,4,64,128]{4,3,2,1,0:T(8,128)}), f32[8,1,4,64,128]{4,3,2,1,0:T(8,128)S(1)}, u32[]{:S(2)}, u32[]{:S(2)}) async-start(f32[8,1,4,64,128]{4,3,2,1,0:T(8,128)} %bitcast.4), calls=%async_computation.1 | async-start | bytes 2097152 | tf_op jit(solution)/shard_map/all_to_all | solution.py:35
  30.0 0.0 copy-done.2
  30.1 0.0 copy-done.3
  30.1 0.1 iota_compare_fusion.3
  30.1 0.0 copy-start.1
  30.1 24.6 %all-to-all-done.1 = f32[8,1,4,64,128]{4,3,2,1,0:T(8,128)S(1)} async-done(((f32[8,1,4,64,128]{4,3,2,1,0:T(8,128)}), f32[8,1,4,64,128]{4,3,2,1,0:T(8,128)S(1)}, u32[]{:S(2)}, u32[]{:S(2)}) %all-to-all-start.1) | async-done | bytes 1048608 | tf_op jit(solution)/shard_map/all_to_all | solution.py:35
  54.8 0.6 convolution_bitcast_fusion.1
  55.4 0.0 copy-done.1
  55.4 6.1 %all_gather.3 = f32[32,5,512]{2,0,1:T(8,128)S(1)} all-gather(f32[32,5,128]{2,0,1:T(8,128)S(1)} %pad_maximum_fusion), channel_id=1, replica_groups=mesh['rows'=8,'cols'=4] {'cols'}, dimensions={2}, use_global_device_ids=true | all-gather | bytes 409600 | tf_op jit(solution)/shard_map/all_gather | solution.py:43
  61.5 1.2 %fusion.9 = f32[32,5,5]{2,1,0:T(8,128)S(1)} fusion(f32[32,5,512]{2,0,1:T(8,128)S(1)} %all_gather.3), kind=kOutput, calls=%fused_computation.12 | convolution fusion | flops 4915200 | bytes 330880 | tf_op jit(solution)/shard_map/bie,bje->bij/dot_general | solution.py:44
  62.8 0.1 slice.16
  62.9 0.1 slice.17
  63.0 0.1 slice.18
  63.1 0.5 slice_reduce_fusion
  63.6 0.7 %copy.33 = f32[32,4,128]{2,1,0:T(4,128)} copy(f32[32,4,128]{2,0,1:T(8,128)S(1)} %convolution_bitcast_fusion.1) | data formatting | bytes 131072
  64.3 0.1 copy.30
  64.3 0.1 copy.31
  64.4 0.1 copy.32
  64.5 0.6 maximum_multiply_fusion
  (9 shorter events, 0.1 us)
Async XLA Ops:
  0.6 0.7 %copy-start = (s32[1,8,4,64]{3,2,1,0:T(4,128)S(1)}, s32[1,8,4,64]{3,2,1,0:T(4,128)}, u32[]{:S(2)}) copy-start(s32[1,8,4,64]{3,2,1,0:T(4,128)} %param.9) | copy-start | bytes 24580
  2.0 13.8 %all-to-all-start = ((s32[8,1,256]{2,1,0:T(1,128)}), s32[8,1,256]{2,1,0:T(1,128)S(1)}, u32[]{:S(2)}, u32[]{:S(2)}) async-start(s32[8,1,256]{2,1,0:T(1,128)} %reshape.23), calls=%async_computation | async-start | bytes 16384 | tf_op jit(solution)/shard_map/all_to_all | solution.py:33
  26.3 3.7 %copy-start.2 = (s32[1,8,4,64]{3,2,1,0:T(4,128)S(1)}, s32[1,8,4,64]{3,2,1,0:T(4,128)}, u32[]{:S(2)}) copy-start(s32[1,8,4,64]{3,2,1,0:T(4,128)} %param.10) | copy-start | bytes 24580
  26.3 3.7 %copy-start.3 = (s32[1,8,4]{1,2,0:T(4,128)S(1)}, s32[1,8,4]{1,2,0:T(4,128)}, u32[]{:S(2)}) copy-start(s32[1,8,4]{1,2,0:T(4,128)} %param.11) | copy-start | bytes 388
  26.3 28.4 %all-to-all-start.1 = ((f32[8,1,4,64,128]{4,3,2,1,0:T(8,128)}), f32[8,1,4,64,128]{4,3,2,1,0:T(8,128)S(1)}, u32[]{:S(2)}, u32[]{:S(2)}) async-start(f32[8,1,4,64,128]{4,3,2,1,0:T(8,128)} %bitcast.4), calls=%async_computation.1 | async-start | bytes 2097152 | tf_op jit(solution)/shard_map/all_to_all | solution.py:35
  30.1 25.2 %copy-start.1 = (f32[32,128]{1,0:T(8,128)S(1)}, f32[32,128]{1,0:T(8,128)}, u32[]{:S(2)}) copy-start(f32[32,128]{1,0:T(8,128)} %param.8) | copy-start | bytes 49156
where the time goes:
time: 65.6 us; the launch traced here: 65.1 us
  waiting for transfers between devices  31.1 us (47%)
  starting transfers between devices  11 us (17%)
  matrix products  11 us (17%)
  blocking collectives  6.13 us (9%)
  local copies, waits for them, and re-layouts  3.74 us (6%)
  other arithmetic  1.37 us (2%)
  between operations  0.74 us (1%)
    all_to_all x1, waiting for transfers between devices, body(): lax.all_to_all(looked[:, None], 'rows', split_axis=0, concat_axis=1, tile...  24.6 us
    dot_general x4, matrix products, one_table(): jnp.einsum('scr,re->sce', selector, table_slice, precision=lax.Precision....  9.16 us
    all_to_all x1, starting transfers between devices, body(): lax.all_to_all(slot_rows, 'rows', split_axis=1, concat_axis=0, tiled=True)  7.28 us
    all_to_all x1, waiting for transfers between devices, body(): lax.all_to_all(slot_rows, 'rows', split_axis=1, concat_axis=0, tiled=True)  6.52 us
    all_gather x1, blocking collectives, body(): complete = lax.all_gather(vectors, 'cols', axis=2, tiled=True)  6.13 us
    all_to_all x1, starting transfers between devices, body(): lax.all_to_all(looked[:, None], 'rows', split_axis=0, concat_axis=1, tile...  3.69 us
    unnamed x12, local copies, waits for them, and re-layouts  2.19 us
  transfers between devices with their start and end apart: 2, of which 2 were waited for; matrix products, arithmetic and copies ran while one was open for 0% of the time, Pallas kernels for 0%

commit v1 on v0

v1 whole, which is shorter than its diff:
```python
import functools

import jax
import jax.numpy as jnp
from jax import lax
from jax.experimental import pallas as pl
from jax.experimental.pallas import tpu as pltpu
from jax.sharding import PartitionSpec as P

MESH = pl.DeviceIdType.MESH
DEAD = -65536


def kernel(
    n,
    cols,
    tables_hbm,
    dense_ref,
    rows_ref,
    examples_ref,
    counts_ref,
    pooled_ref,
    inter_ref,
    table_buf,
    split_buf,
    id_send,
    id_recv,
    pair_keep,
    pair_send,
    pair_recv,
    far_send,
    far_recv,
    gram_recv,
    gram_send,
    table_sem,
    id_ssem,
    id_rsem,
    pair_ssem,
    pair_rsem,
    far_ssem,
    far_rsem,
    gram_ssem,
    gram_rsem,
):
    tables, range_rows, width = table_buf.shape
    here = dense_ref.shape[0]
    cap = rows_ref.shape[3]
    far = n // 2
    me = lax.axis_index("rows")
    col = lax.axis_index("cols")
    hi, lo = me // 2, me % 2
    mate = hi * 2 + (1 - lo)

    load = pltpu.make_async_copy(tables_hbm, table_buf, table_sem)
    load.start()

    barrier = pltpu.get_barrier_semaphore()
    for j in range(1, n):
        pl.semaphore_signal(barrier, inc=1, device_id={"rows": (me + j) % n}, device_id_type=MESH)
    for j in range(1, cols):
        pl.semaphore_signal(barrier, inc=1, device_id={"cols": (col + j) % cols}, device_id_type=MESH)

    slot = lax.broadcasted_iota(jnp.int32, (tables, cap), 1)
    table_id = lax.broadcasted_iota(jnp.int32, (tables, cap), 0)
    for p in range(n):
        count = jnp.full((tables, cap), counts_ref[0, p, 0], jnp.int32)
        for t in range(1, tables):
            count = jnp.where(table_id == t, counts_ref[0, p, t], count)
        rows_p = rows_ref[0, p]
        ex_p = jnp.where(slot < count, examples_ref[0, p], DEAD)
        id_send[p, 0:tables, :] = jnp.concatenate([rows_p, rows_p], axis=1)
        id_send[p, tables : 2 * tables, :] = jnp.concatenate([ex_p, ex_p], axis=1)

    pl.semaphore_wait(barrier, n - 1 + cols - 1)

    def id_copy(dst):
        return pltpu.make_async_remote_copy(
            src_ref=id_send.at[dst],
            dst_ref=id_recv.at[me],
            send_sem=id_ssem.at[dst],
            recv_sem=id_rsem.at[me],
            device_id={"rows": dst},
            device_id_type=MESH,
        )

    def id_wait(src):
        pltpu.make_async_remote_copy(
            src_ref=id_send.at[src],
            dst_ref=id_recv.at[src],
            send_sem=id_ssem.at[src],
            recv_sem=id_rsem.at[src],
            device_id={"rows": src},
            device_id_type=MESH,
        ).wait_recv()

    for j in range(1, far):
        dst_hi = (hi + far - j) % far
        id_copy(dst_hi * 2 + lo).start()
        id_copy(dst_hi * 2 + (1 - lo)).start()
    id_copy(mate).start()
    id_recv[me] = id_send[me]

    load.wait()
    for t in range(tables):
        whole = table_buf[t]
        high = whole.astype(jnp.bfloat16)
        split_buf[t, :, 0:width] = high
        split_buf[t, :, width : 2 * width] = (whole - high.astype(jnp.float32)).astype(jnp.bfloat16)

    first_half = lax.broadcasted_iota(jnp.int32, (tables, 2 * cap), 1) < cap
    offset = jnp.where(first_half, lo * here, (1 - lo) * here)
    row_iota = lax.broadcasted_iota(jnp.int32, (range_rows, 2 * cap), 0)
    ex_iota = lax.broadcasted_iota(jnp.int32, (2 * here, 2 * cap), 0)

    def group_of(k):
        return (hi + 1 + k) % far

    def pair_copy(g):
        return pltpu.make_async_remote_copy(
            src_ref=pair_send.at[g],
            dst_ref=pair_recv.at[g],
            send_sem=pair_ssem.at[g],
            recv_sem=pair_rsem.at[g],
            device_id={"rows": mate},
            device_id_type=MESH,
        )

    def far_copy(g):
        return pltpu.make_async_remote_copy(
            src_ref=far_send.at[g],
            dst_ref=far_recv.at[hi],
            send_sem=far_ssem.at[g],
            recv_sem=far_rsem.at[hi],
            device_id={"rows": g * 2 + lo},
            device_id_type=MESH,
        )

    def far_wait(g):
        pltpu.make_async_remote_copy(
            src_ref=far_send.at[g],
            dst_ref=far_recv.at[g],
            send_sem=far_ssem.at[g],
            recv_sem=far_rsem.at[g],
            device_id={"rows": g * 2 + lo},
            device_id_type=MESH,
        ).wait_recv()

    def compute(g):
        even = id_recv[g * 2]
        odd = id_recv[g * 2 + 1]
        row_of = jnp.where(first_half, even[0:tables], odd[0:tables])
        code = jnp.where(first_half, even[tables : 2 * tables], odd[tables : 2 * tables]) + offset
        for t in range(tables):
            row_hot = jnp.where(row_iota == row_of[t : t + 1], 1.0, 0.0).astype(jnp.bfloat16)
            ex_hot = jnp.where(ex_iota == code[t : t + 1], 1.0, 0.0).astype(jnp.bfloat16)
            hits = lax.dot_general(
                ex_hot, row_hot, (((1,), (1,)), ((), ())), preferred_element_type=jnp.float32
            ).astype(jnp.bfloat16)
            both = jnp.dot(hits, split_buf[t], preferred_element_type=jnp.float32)
            part = both[:, 0:width] + both[:, width : 2 * width]
            pair_keep[g, t] = part[0:here]
            pair_send[g, t] = part[here : 2 * here]
        pair_copy(g).start()

    def forward(g):
        pair_copy(g).wait_recv()
        far_send[g] = pair_keep[g] + pair_recv[g]
        far_copy(g).start()

    def remote_group(g):
        id_wait(g * 2)
        id_wait(g * 2 + 1)
        compute(g)

    remote_group(group_of(0))
    if far <= 8:
        for k in range(1, far - 1):
            remote_group(group_of(k))
            forward(group_of(k - 1))
    else:

        @pl.loop(1, far - 1)
        def _(k):
            remote_group(group_of(k))
            forward(group_of(k - 1))

    id_wait(mate)
    compute(hi)
    forward(group_of(far - 2))

    pair_copy(hi).wait_recv()
    total = pair_keep[hi] + pair_recv[hi]
    for k in range(far - 1):
        g = (hi + far - 1 - k) % far
        far_wait(g)
        total = total + far_recv[g]

    vectors = [dense_ref[...]] + [total[t] for t in range(tables)]
    for t in range(tables):
        pooled_ref[:, t, :] = total[t]
    lane = lax.broadcasted_iota(jnp.int32, (here, 128), 1)
    gram = jnp.zeros((here, 128), jnp.float32)
    pair = 0
    for i in range(tables + 1):
        for j in range(i + 1, tables + 1):
            inner = jnp.sum(vectors[i] * vectors[j], axis=1, keepdims=True)
            gram = jnp.where(lane == pair, inner, gram)
            pair += 1
    gram_send[...] = gram
    gram_recv[col] = gram

    def gram_copy(j):
        return pltpu.make_async_remote_copy(
            src_ref=gram_send,
            dst_ref=gram_recv.at[col],
            send_sem=gram_ssem.at[j],
            recv_sem=gram_rsem.at[col],
            device_id={"cols": (col + j) % cols},
            device_id_type=MESH,
        )

    for j in range(1, cols):
        gram_copy(j).start()
    for j in range(1, cols):
        src = (col + j) % cols
        pltpu.make_async_remote_copy(
            src_ref=gram_send,
            dst_ref=gram_recv.at[src],
            send_sem=gram_ssem.at[j],
            recv_sem=gram_rsem.at[src],
            device_id={"cols": src},
            device_id_type=MESH,
        ).wait_recv()
    summed = gram_recv[0]
    for c in range(1, cols):
        summed = summed + gram_recv[c]
    inter_ref[...] = (summed * (width * cols) ** (-0.5))[:, 0:pair]

    for j in range(1, n):
        id_copy((me + j) % n).wait_send()
    for g in range(far):
        pair_copy(g).wait_send()
    for j in range(1, far):
        far_copy((hi + j) % far).wait_send()
    for j in range(1, cols):
        gram_copy(j).wait_send()


def body(n, cols, tables, dense_features, slot_rows, slot_examples, slot_counts):
    count, range_rows, width = tables.shape
    here = dense_features.shape[0]
    cap = slot_rows.shape[3]
    far = n // 2
    pairs = (count + 1) * count // 2
    vmem = pl.BlockSpec(memory_space=pltpu.VMEM)
    block = (far, count, here, width)
    return pl.pallas_call(
        functools.partial(kernel, n, cols),
        out_shape=(
            jax.ShapeDtypeStruct((here, count, width), jnp.float32),
            jax.ShapeDtypeStruct((here, pairs), jnp.float32),
        ),
        in_specs=[
            pl.BlockSpec(memory_space=pl.ANY),
            vmem,
            vmem,
            vmem,
            pl.BlockSpec(memory_space=pltpu.SMEM),
        ],
        out_specs=(vmem, vmem),
        scratch_shapes=[
            pltpu.VMEM((count, range_rows, width), jnp.float32),
            pltpu.VMEM((count, range_rows, 2 * width), jnp.bfloat16),
            pltpu.VMEM((n, 2 * count, 2 * cap), jnp.int32),
            pltpu.VMEM((n, 2 * count, 2 * cap), jnp.int32),
            pltpu.VMEM(block, jnp.float32),
            pltpu.VMEM(block, jnp.float32),
            pltpu.VMEM(block, jnp.float32),
            pltpu.VMEM(block, jnp.float32),
            pltpu.VMEM(block, jnp.float32),
            pltpu.VMEM((cols, here, 128), jnp.float32),
            pltpu.VMEM((here, 128), jnp.float32),
            pltpu.SemaphoreType.DMA,
            pltpu.SemaphoreType.DMA((n,)),
            pltpu.SemaphoreType.DMA((n,)),
            pltpu.SemaphoreType.DMA((far,)),
            pltpu.SemaphoreType.DMA((far,)),
            pltpu.SemaphoreType.DMA((far,)),
            pltpu.SemaphoreType.DMA((far,)),
            pltpu.SemaphoreType.DMA((cols,)),
            pltpu.SemaphoreType.DMA((cols,)),
        ],
        compiler_params=pltpu.CompilerParams(collective_id=0, has_side_effects=True),
    )(tables, dense_features, slot_rows, slot_examples, slot_counts)


def solution(mesh):
    placed = (
        P(None, "rows", "cols"),
        P("rows", "cols"),
        P("rows", None, None, None),
        P("rows", None, None, None),
        P("rows", None, None),
    )
    return jax.shard_map(
        functools.partial(body, mesh.shape["rows"], mesh.shape["cols"]),
        mesh=mesh,
        in_specs=placed,
        out_specs=(P("rows", None, "cols"), P("rows", None)),
        check_vma=False,
    )
```

time: 65.6 us -> 29.6 us (0.45)
  waiting for transfers between devices: 31.1 us -> 0 us
  Pallas kernels: 0 us -> 24.4 us
  matrix products: 11 us -> 0 us
  starting transfers between devices: 11 us -> 0 us
  blocking collectives: 6.13 us -> 0 us
  other arithmetic: 1.37 us -> 0 us
    all_to_all x2 -> x0, waiting for transfers between devices: 31.1 us -> none  [the longest x1 24.6 us: body(): lax.all_to_all(looked[:, None], 'rows', split_axis=0, concat_axis=1, tile...]
    pallas_call x0 -> x1, Pallas kernels: none -> 24.4 us  [body(): pl.pallas_call(functools.partial(kernel, n, cols), out_shape=(jax.ShapeDt...]
    dot_general x6 -> x0, matrix products: 11 us -> none  [the longest x4 9.16 us: one_table(): jnp.einsum('scr,re->sce', selector, table_slice, precision=lax.Precision....]
    all_to_all x2 -> x0, starting transfers between devices: 11 us -> none  [the longest x1 7.28 us: body(): lax.all_to_all(slot_rows, 'rows', split_axis=1, concat_axis=0, tiled=True)]
    all_gather x1 -> x0, blocking collectives: 6.13 us -> none  [body(): complete = lax.all_gather(vectors, 'cols', axis=2, tiled=True)]
    pallas_call x0 -> x1, local copies, waits for them, and re-layouts: none -> 1.39 us  [body(): pl.pallas_call(functools.partial(kernel, n, cols), out_shape=(jax.ShapeDt...]
    slice x7 -> x0, local copies, waits for them, and re-layouts: 1 us -> none  [upper_pairs(): pieces = [gram_matrix[:, first, first + 1:] for first in range(count - 1)]]
    all_to_all x1 -> x0, other arithmetic: 0.67 us -> none  [body(): lax.all_to_all(slot_rows, 'rows', split_axis=1, concat_axis=0, tiled=True)]
  transfers between devices with their start and end apart: 2 -> 0, of which waited for: 2 -> 0; matrix products, arithmetic and copies ran while one was open for 0% -> 0% of each run, Pallas kernels for 0% -> 0%
where the time goes in v1:
time: 29.6 us; the launch traced here: 29.3 us
  Pallas kernels  24.4 us (82%)
  local copies, waits for them, and re-layouts  4.21 us (14%)
  between operations  0.64 us (2%)
    pallas_call x1, Pallas kernels, body(): pl.pallas_call(functools.partial(kernel, n, cols), out_shape=(jax.ShapeDt...  24.4 us
    unnamed x2, local copies, waits for them, and re-layouts  2.82 us
    pallas_call x1, local copies, waits for them, and re-layouts, body(): pl.pallas_call(functools.partial(kernel, n, cols), out_shape=(jax.ShapeDt...  1.39 us

profile of v1, /device:TPU:0, one launch (start us, length us, event | category | flops | bytes accessed | tf_op | source)
XLA Modules:
  0.0 29.3 jit_solution(18009169480999270923)
XLA Ops:
  0.6 1.3 %copy.7.counts_ref = s32[1,8,4]{2,1,0:T(8,128)} copy(s32[1,8,4]{1,2,0:T(4,128)} %param.9) | data formatting | bytes 256 | tf_op args[4]
  2.0 24.4 %shard_map.68 = (f32[32,4,128]{2,1,0:T(4,128)}, f32[32,10]{1,0:T(8,128)}) custom-call(f32[4,512,128]{2,1,0:T(8,128)} %tables_hbm.1, f32[32,128]{1,0:T(8,128)} %dense_ref.1, s32[1,8,4,64]{3,2,1,0:T(4,128)} %rows_ref.1, s32[1,8,4,64]{3,2,1,0:T(4,128)} %examples_ref.1, s32[1,8,4]{2,1,0:T(8,128)} %copy.7.counts_ref), custom_call_target="tpu_custom_call" | custom-call | tf_op jit(solution)/shard_map/pallas_call | solution.py:257
  26.4 1.4 %copy.8 = f32[32,10]{0,1:T(8,128)} copy(f32[32,10]{1,0:T(8,128)} %get-tuple-element.3) | data formatting | bytes 2560 | tf_op jit(solution)/shard_map/pallas_call | solution.py:257
  27.8 1.5 %copy.10 = f32[32,4,128]{2,1,0:T(4,128)} copy(f32[32,4,128]{2,1,0:T(4,128)} %get-tuple-element.6) | data formatting | bytes 131072

commit v2 on v1

--- a/solution.py
+++ b/solution.py
@@ -8,6 +8,7 @@
 from jax.sharding import PartitionSpec as P
 
 MESH = pl.DeviceIdType.MESH
+CHUNKS = 2
 DEAD = -65536
 
 
@@ -15,12 +16,17 @@
     n,
     cols,
     tables_hbm,
+    dense_hbm,
+    rows_hbm,
+    examples_hbm,
+    counts_hbm,
+    pooled_hbm,
+    inter_ref,
     dense_ref,
     rows_ref,
     examples_ref,
     counts_ref,
     pooled_ref,
-    inter_ref,
     table_buf,
     split_buf,
     id_send,
@@ -32,7 +38,7 @@
     far_recv,
     gram_recv,
     gram_send,
-    table_sem,
+    load_sem,
     id_ssem,
     id_rsem,
     pair_ssem,
@@ -41,18 +47,22 @@
     far_rsem,
     gram_ssem,
     gram_rsem,
+    store_sem,
 ):
     tables, range_rows, width = table_buf.shape
     here = dense_ref.shape[0]
     cap = rows_ref.shape[3]
     far = n // 2
+    chunks = pair_ssem.shape[1]
+    step = tables // chunks
     me = lax.axis_index("rows")
     col = lax.axis_index("cols")
     hi, lo = me // 2, me % 2
     mate = hi * 2 + (1 - lo)
 
-    load = pltpu.make_async_copy(tables_hbm, table_buf, table_sem)
-    load.start()
+    sources = (counts_hbm, rows_hbm, examples_hbm, tables_hbm, dense_hbm)
+    targets = (counts_ref, rows_ref, examples_ref, table_buf, dense_ref)
+    loads = [pltpu.make_async_copy(a, b, load_sem.at[i]) for i, (a, b) in enumerate(zip(sources, targets))]
 
     barrier = pltpu.get_barrier_semaphore()
     for j in range(1, n):
@@ -60,18 +70,31 @@
     for j in range(1, cols):
         pl.semaphore_signal(barrier, inc=1, device_id={"cols": (col + j) % cols}, device_id_type=MESH)
 
+    for load in loads:
+        load.start()
+
     slot = lax.broadcasted_iota(jnp.int32, (tables, cap), 1)
     table_id = lax.broadcasted_iota(jnp.int32, (tables, cap), 0)
+    for load in loads[:3]:
+        load.wait()
     for p in range(n):
-        count = jnp.full((tables, cap), counts_ref[0, p, 0], jnp.int32)
+        count = jnp.full((tables, cap), counts_ref[0, 0, p], jnp.int32)
         for t in range(1, tables):
-            count = jnp.where(table_id == t, counts_ref[0, p, t], count)
+            count = jnp.where(table_id == t, counts_ref[0, t, p], count)
         rows_p = rows_ref[0, p]
         ex_p = jnp.where(slot < count, examples_ref[0, p], DEAD)
         id_send[p, 0:tables, :] = jnp.concatenate([rows_p, rows_p], axis=1)
         id_send[p, tables : 2 * tables, :] = jnp.concatenate([ex_p, ex_p], axis=1)
 
     pl.semaphore_wait(barrier, n - 1 + cols - 1)
+
+    high_half = (2 * hi) // far
+    low_hi = hi * (1 - high_half) + (far - 1 - hi) * high_half
+
+    def group_of(k):
+        beyond = (2 * (far - 1) - k - low_hi) // far
+        g = far - 2 - k + beyond
+        return g * (1 - high_half) + (far - 1 - g) * high_half
 
     def id_copy(dst):
         return pltpu.make_async_remote_copy(
@@ -93,14 +116,14 @@
             device_id_type=MESH,
         ).wait_recv()
 
-    for j in range(1, far):
-        dst_hi = (hi + far - j) % far
+    for k in range(far - 1):
+        dst_hi = group_of(k)
         id_copy(dst_hi * 2 + lo).start()
         id_copy(dst_hi * 2 + (1 - lo)).start()
     id_copy(mate).start()
     id_recv[me] = id_send[me]
 
-    load.wait()
+    loads[3].wait()
     for t in range(tables):
         whole = table_buf[t]
         high = whole.astype(jnp.bfloat16)
@@ -112,35 +135,35 @@
     row_iota = lax.broadcasted_iota(jnp.int32, (range_rows, 2 * cap), 0)
     ex_iota = lax.broadcasted_iota(jnp.int32, (2 * here, 2 * cap), 0)
 
-    def group_of(k):
-        return (hi + 1 + k) % far
-
-    def pair_copy(g):
+    def pair_copy(g, c):
+        piece = pl.ds(c * step, step)
         return pltpu.make_async_remote_copy(
-            src_ref=pair_send.at[g],
-            dst_ref=pair_recv.at[g],
-            send_sem=pair_ssem.at[g],
-            recv_sem=pair_rsem.at[g],
+            src_ref=pair_send.at[g, piece],
+            dst_ref=pair_recv.at[g, piece],
+            send_sem=pair_ssem.at[g, c],
+            recv_sem=pair_rsem.at[g, c],
             device_id={"rows": mate},
             device_id_type=MESH,
         )
 
-    def far_copy(g):
+    def far_copy(g, c):
+        piece = pl.ds(c * step, step)
         return pltpu.make_async_remote_copy(
-            src_ref=far_send.at[g],
-            dst_ref=far_recv.at[hi],
-            send_sem=far_ssem.at[g],
-            recv_sem=far_rsem.at[hi],
+            src_ref=far_send.at[g, piece],
+            dst_ref=far_recv.at[hi, piece],
+            send_sem=far_ssem.at[g, c],
+            recv_sem=far_rsem.at[hi, c],
             device_id={"rows": g * 2 + lo},
             device_id_type=MESH,
         )
 
-    def far_wait(g):
+    def far_wait(g, c):
+        piece = pl.ds(c * step, step)
         pltpu.make_async_remote_copy(
-            src_ref=far_send.at[g],
-            dst_ref=far_recv.at[g],
-            send_sem=far_ssem.at[g],
-            recv_sem=far_rsem.at[g],
+            src_ref=far_send.at[g, piece],
+            dst_ref=far_recv.at[g, piece],
+            send_sem=far_ssem.at[g, c],
+            recv_sem=far_rsem.at[g, c],
             device_id={"rows": g * 2 + lo},
             device_id_type=MESH,
         ).wait_recv()
@@ -160,12 +183,15 @@
             part = both[:, 0:width] + both[:, width : 2 * width]
             pair_keep[g, t] = part[0:here]
             pair_send[g, t] = part[here : 2 * here]
-        pair_copy(g).start()
+            if (t + 1) % step == 0:
+                pair_copy(g, t // step).start()
 
     def forward(g):
-        pair_copy(g).wait_recv()
-        far_send[g] = pair_keep[g] + pair_recv[g]
-        far_copy(g).start()
+        for c in range(chunks):
+            pair_copy(g, c).wait_recv()
+            piece = pl.ds(c * step, step)
+            far_send[g, piece] = pair_keep[g, piece] + pair_recv[g, piece]
+            far_copy(g, c).start()
 
     def remote_group(g):
         id_wait(g * 2)
@@ -188,16 +214,21 @@
     compute(hi)
     forward(group_of(far - 2))
 
-    pair_copy(hi).wait_recv()
+    for c in range(chunks):
+        pair_copy(hi, c).wait_recv()
     total = pair_keep[hi] + pair_recv[hi]
     for k in range(far - 1):
-        g = (hi + far - 1 - k) % far
-        far_wait(g)
+        g = group_of(far - 2 - k)
+        for c in range(chunks):
+            far_wait(g, c)
         total = total + far_recv[g]
 
-    vectors = [dense_ref[...]] + [total[t] for t in range(tables)]
     for t in range(tables):
         pooled_ref[:, t, :] = total[t]
+    store = pltpu.make_async_copy(pooled_ref, pooled_hbm, store_sem)
+    store.start()
+    loads[4].wait()
+    vectors = [dense_ref[...]] + [total[t] for t in range(tables)]
     lane = lax.broadcasted_iota(jnp.int32, (here, 128), 1)
     gram = jnp.zeros((here, 128), jnp.float32)
     pair = 0
@@ -206,6 +237,7 @@
             inner = jnp.sum(vectors[i] * vectors[j], axis=1, keepdims=True)
             gram = jnp.where(lane == pair, inner, gram)
             pair += 1
+    gram = gram.T[0 : gram_send.shape[0]]
     gram_send[...] = gram
     gram_recv[col] = gram
 
@@ -234,16 +266,18 @@
     summed = gram_recv[0]
     for c in range(1, cols):
         summed = summed + gram_recv[c]
-    inter_ref[...] = (summed * (width * cols) ** (-0.5))[:, 0:pair]
+    inter_ref[...] = (summed * (width * cols) ** (-0.5))[0:pair]
 
     for j in range(1, n):
         id_copy((me + j) % n).wait_send()
-    for g in range(far):
-        pair_copy(g).wait_send()
-    for j in range(1, far):
-        far_copy((hi + j) % far).wait_send()
+    for c in range(chunks):
+        for g in range(far):
+            pair_copy(g, c).wait_send()
+        for j in range(1, far):
+            far_copy((hi + j) % far, c).wait_send()
     for j in range(1, cols):
         gram_copy(j).wait_send()
+    store.wait()
 
 
 def body(n, cols, tables, dense_features, slot_rows, slot_examples, slot_counts):
@@ -254,21 +288,23 @@
     pairs = (count + 1) * count // 2
     vmem = pl.BlockSpec(memory_space=pltpu.VMEM)
     block = (far, count, here, width)
-    return pl.pallas_call(
+    chunks = CHUNKS
+    any_space = pl.BlockSpec(memory_space=pl.ANY)
+    pair_rows = -(-pairs // 8) * 8
+    pooled, inter = pl.pallas_call(
         functools.partial(kernel, n, cols),
         out_shape=(
             jax.ShapeDtypeStruct((here, count, width), jnp.float32),
-            jax.ShapeDtypeStruct((here, pairs), jnp.float32),
+            jax.ShapeDtypeStruct((pairs, here), jnp.float32),
         ),
-        in_specs=[
-            pl.BlockSpec(memory_space=pl.ANY),
-            vmem,
-            vmem,
-            vmem,
-            pl.BlockSpec(memory_space=pltpu.SMEM),
-        ],
-        out_specs=(vmem, vmem),
+        in_specs=[any_space] * 5,
+        out_specs=(any_space, vmem),
         scratch_shapes=[
+            pltpu.VMEM((here, width), jnp.float32),
+            pltpu.VMEM(slot_rows.shape, jnp.int32),
+            pltpu.VMEM(slot_rows.shape, jnp.int32),
+            pltpu.SMEM((1, count, n), jnp.int32),
+            pltpu.VMEM((here, count, width), jnp.float32),
             pltpu.VMEM((count, range_rows, width), jnp.float32),
             pltpu.VMEM((count, range_rows, 2 * width), jnp.bfloat16),
             pltpu.VMEM((n, 2 * count, 2 * cap), jnp.int32),
@@ -278,20 +314,22 @@
             pltpu.VMEM(block, jnp.float32),
             pltpu.VMEM(block, jnp.float32),
             pltpu.VMEM(block, jnp.float32),
-            pltpu.VMEM((cols, here, 128), jnp.float32),
-            pltpu.VMEM((here, 128), jnp.float32),
-            pltpu.SemaphoreType.DMA,
+            pltpu.VMEM((cols, pair_rows, here), jnp.float32),
+            pltpu.VMEM((pair_rows, here), jnp.float32),
+            pltpu.SemaphoreType.DMA((5,)),
             pltpu.SemaphoreType.DMA((n,)),
             pltpu.SemaphoreType.DMA((n,)),
-            pltpu.SemaphoreType.DMA((far,)),
-            pltpu.SemaphoreType.DMA((far,)),
-            pltpu.SemaphoreType.DMA((far,)),
-            pltpu.SemaphoreType.DMA((far,)),
+            pltpu.SemaphoreType.DMA((far, chunks)),
+            pltpu.SemaphoreType.DMA((far, chunks)),
+            pltpu.SemaphoreType.DMA((far, chunks)),
+            pltpu.SemaphoreType.DMA((far, chunks)),
             pltpu.SemaphoreType.DMA((cols,)),
             pltpu.SemaphoreType.DMA((cols,)),
+            pltpu.SemaphoreType.DMA,
         ],
         compiler_params=pltpu.CompilerParams(collective_id=0, has_side_effects=True),
-    )(tables, dense_features, slot_rows, slot_examples, slot_counts)
+    )(tables, dense_features, slot_rows, slot_examples, slot_counts.transpose(0, 2, 1))
+    return pooled, inter.T
 
 
 def solution(mesh):

time: 29.6 us -> 26.1 us (0.88)
  local copies, waits for them, and re-layouts: 4.21 us -> 2.08 us
  Pallas kernels: 24.4 us -> 23.2 us
    pallas_call x1 -> x0, local copies, waits for them, and re-layouts: 1.39 us -> none  [body(): pl.pallas_call(functools.partial(kernel, n, cols), out_shape=(jax.ShapeDt...]
    pallas_call x1, Pallas kernels: 24.4 us -> 23.2 us  [body(): pl.pallas_call(functools.partial(kernel, n, cols), out_shape=(jax.ShapeDt...]
    unnamed x2 -> x4, local copies, waits for them, and re-layouts: 2.82 us -> 2.08 us
where the time goes in v2:
time: 26.1 us; the launch traced here: 26 us
  Pallas kernels  23.2 us (89%)
  local copies, waits for them, and re-layouts  2.08 us (8%)
  between operations  0.65 us (2%)
    pallas_call x1, Pallas kernels, body(): pl.pallas_call(functools.partial(kernel, n, cols), out_shape=(jax.ShapeDt...  23.2 us
    unnamed x4, local copies, waits for them, and re-layouts  2.08 us

profile of v2, /device:TPU:0, one launch (start us, length us, event | category | flops | bytes accessed | tf_op | source)
XLA Modules:
  0.0 26.0 jit_solution(16855630042561191991)
XLA Ops:
  0.6 23.2 %shard_map.68 = (f32[32,4,128]{2,1,0:T(4,128)}, f32[10,32]{1,0:T(8,128)}) custom-call(f32[4,512,128]{2,1,0:T(8,128)} %tables_hbm.1, f32[32,128]{1,0:T(8,128)} %dense_hbm.1, s32[1,8,4,64]{3,2,1,0:T(4,128)} %rows_hbm.1, s32[1,8,4,64]{3,2,1,0:T(4,128)} %examples_hbm.1, s32[1,4,8]{2,1,0:T(4,128)} %bitcast.3), custom_call_target="tpu_custom_call" | custom-call | tf_op jit(solution)/shard_map/pallas_call | solution.py:294
  23.9 0.0 copy-start
  23.9 1.5 %copy.9 = f32[32,4,128]{2,1,0:T(4,128)} copy(f32[32,4,128]{2,1,0:T(4,128)} %get-tuple-element.8) | data formatting | bytes 131072
  25.4 0.0 copy-done
  25.4 0.6 %copy.10 = f32[32,10]{0,1:T(8,128)} copy(f32[32,10]{0,1:T(8,128)S(1)} %bitcast.2) | data formatting | bytes 2560
Async XLA Ops:
  23.9 1.5 %copy-start = (f32[10,32]{1,0:T(8,128)S(1)}, f32[10,32]{1,0:T(8,128)}, u32[]{:S(2)}) copy-start(f32[10,32]{1,0:T(8,128)} %get-tuple-element.5) | copy-start | bytes 3844

commit v3 on v2

--- a/solution.py
+++ b/solution.py
@@ -20,13 +20,12 @@
     rows_hbm,
     examples_hbm,
     counts_hbm,
-    pooled_hbm,
+    pooled_ref,
     inter_ref,
     dense_ref,
     rows_ref,
     examples_ref,
     counts_ref,
-    pooled_ref,
     table_buf,
     split_buf,
     id_send,
@@ -47,7 +46,6 @@
     far_rsem,
     gram_ssem,
     gram_rsem,
-    store_sem,
 ):
     tables, range_rows, width = table_buf.shape
     here = dense_ref.shape[0]
@@ -225,8 +223,6 @@
 
     for t in range(tables):
         pooled_ref[:, t, :] = total[t]
-    store = pltpu.make_async_copy(pooled_ref, pooled_hbm, store_sem)
-    store.start()
     loads[4].wait()
     vectors = [dense_ref[...]] + [total[t] for t in range(tables)]
     lane = lax.broadcasted_iota(jnp.int32, (here, 128), 1)
@@ -277,7 +273,6 @@
             far_copy((hi + j) % far, c).wait_send()
     for j in range(1, cols):
         gram_copy(j).wait_send()
-    store.wait()
 
 
 def body(n, cols, tables, dense_features, slot_rows, slot_examples, slot_counts):
@@ -294,17 +289,16 @@
     pooled, inter = pl.pallas_call(
         functools.partial(kernel, n, cols),
         out_shape=(
-            jax.ShapeDtypeStruct((here, count, width), jnp.float32),
-            jax.ShapeDtypeStruct((pairs, here), jnp.float32),
+            pltpu.VMEM((here, count, width), jnp.float32),
+            pltpu.VMEM((pairs, here), jnp.float32),
         ),
         in_specs=[any_space] * 5,
-        out_specs=(any_space, vmem),
+        out_specs=(vmem, vmem),
         scratch_shapes=[
             pltpu.VMEM((here, width), jnp.float32),
             pltpu.VMEM(slot_rows.shape, jnp.int32),
             pltpu.VMEM(slot_rows.shape, jnp.int32),
             pltpu.SMEM((1, count, n), jnp.int32),
-            pltpu.VMEM((here, count, width), jnp.float32),
             pltpu.VMEM((count, range_rows, width), jnp.float32),
             pltpu.VMEM((count, range_rows, 2 * width), jnp.bfloat16),
             pltpu.VMEM((n, 2 * count, 2 * cap), jnp.int32),
@@ -325,7 +319,6 @@
             pltpu.SemaphoreType.DMA((far, chunks)),
             pltpu.SemaphoreType.DMA((cols,)),
             pltpu.SemaphoreType.DMA((cols,)),
-            pltpu.SemaphoreType.DMA,
         ],
         compiler_params=pltpu.CompilerParams(collective_id=0, has_side_effects=True),
     )(tables, dense_features, slot_rows, slot_examples, slot_counts.transpose(0, 2, 1))

time: 26.1 us -> 24.7 us (0.946)
  local copies, waits for them, and re-layouts: 2.08 us -> 1.23 us
  Pallas kernels: 23.2 us -> 22.6 us
    unnamed x4 -> x2, local copies, waits for them, and re-layouts: 2.08 us -> 1.23 us
    pallas_call x1, Pallas kernels: 23.2 us -> 22.6 us  [body(): pl.pallas_call(functools.partial(kernel, n, cols), out_shape=(pltpu.VMEM(...]
where the time goes in v3:
time: 24.7 us; the launch traced here: 24.5 us
  Pallas kernels  22.6 us (91%)
  local copies, waits for them, and re-layouts  1.23 us (5%)
  between operations  0.64 us (3%)
    pallas_call x1, Pallas kernels, body(): pl.pallas_call(functools.partial(kernel, n, cols), out_shape=(pltpu.VMEM(...  22.6 us
    unnamed x2, local copies, waits for them, and re-layouts  1.23 us

profile of v3, /device:TPU:0, one launch (start us, length us, event | category | flops | bytes accessed | tf_op | source)
XLA Modules:
  0.0 24.5 jit_solution(7906902696550039318)
XLA Ops:
  0.6 22.6 %shard_map.68 = (f32[32,4,128]{2,1,0:T(4,128)S(1)}, f32[10,32]{1,0:T(8,128)S(1)}) custom-call(f32[4,512,128]{2,1,0:T(8,128)} %tables_hbm.1, f32[32,128]{1,0:T(8,128)} %dense_hbm.1, s32[1,8,4,64]{3,2,1,0:T(4,128)} %rows_hbm.1, s32[1,8,4,64]{3,2,1,0:T(4,128)} %examples_hbm.1, s32[1,4,8]{2,1,0:T(4,128)} %bitcast.3), custom_call_target="tpu_custom_call" | custom-call | tf_op jit(solution)/shard_map/pallas_call | solution.py:289
  23.3 0.6 %copy.9 = f32[32,4,128]{2,1,0:T(4,128)} copy(f32[32,4,128]{2,1,0:T(4,128)S(1)} %get-tuple-element.6) | data formatting | bytes 131072
  23.9 0.6 %copy.10 = f32[32,10]{0,1:T(8,128)} copy(f32[32,10]{0,1:T(8,128)S(1)} %bitcast.2) | data formatting | bytes 2560

commit v4 on v3

--- a/solution.py
+++ b/solution.py
@@ -35,6 +35,7 @@
     pair_recv,
     far_send,
     far_recv,
+    near_recv,
     gram_recv,
     gram_send,
     load_sem,
@@ -44,6 +45,8 @@
     pair_rsem,
     far_ssem,
     far_rsem,
+    near_ssem,
+    near_rsem,
     gram_ssem,
     gram_rsem,
 ):
@@ -86,13 +89,8 @@
 
     pl.semaphore_wait(barrier, n - 1 + cols - 1)
 
-    high_half = (2 * hi) // far
-    low_hi = hi * (1 - high_half) + (far - 1 - hi) * high_half
-
     def group_of(k):
-        beyond = (2 * (far - 1) - k - low_hi) // far
-        g = far - 2 - k + beyond
-        return g * (1 - high_half) + (far - 1 - g) * high_half
+        return (hi // 2 + 1 + k // 2) % (far // 2) * 2 + (hi + 1 + k) % 2
 
     def id_copy(dst):
         return pltpu.make_async_remote_copy(
@@ -166,7 +164,19 @@
             device_id_type=MESH,
         ).wait_recv()
 
-    def compute(g):
+    near = hi + 1 - 2 * (hi % 2)
+
+    def near_copy(same):
+        return pltpu.make_async_remote_copy(
+            src_ref=pair_keep.at[near] if same else pair_send.at[near],
+            dst_ref=near_recv.at[0 if same else 1],
+            send_sem=near_ssem.at[0 if same else 1],
+            recv_sem=near_rsem.at[0 if same else 1],
+            device_id={"rows": near * 2 + (lo if same else 1 - lo)},
+            device_id_type=MESH,
+        )
+
+    def compute(g, paired=True):
         even = id_recv[g * 2]
         odd = id_recv[g * 2 + 1]
         row_of = jnp.where(first_half, even[0:tables], odd[0:tables])
@@ -181,7 +191,7 @@
             part = both[:, 0:width] + both[:, width : 2 * width]
             pair_keep[g, t] = part[0:here]
             pair_send[g, t] = part[here : 2 * here]
-            if (t + 1) % step == 0:
+            if paired and (t + 1) % step == 0:
                 pair_copy(g, t // step).start()
 
     def forward(g):
@@ -198,25 +208,33 @@
 
     remote_group(group_of(0))
     if far <= 8:
-        for k in range(1, far - 1):
+        for k in range(1, far - 2):
             remote_group(group_of(k))
             forward(group_of(k - 1))
     else:
 
-        @pl.loop(1, far - 1)
+        @pl.loop(1, far - 2)
         def _(k):
             remote_group(group_of(k))
             forward(group_of(k - 1))
 
+    id_wait(near * 2)
+    id_wait(near * 2 + 1)
+    compute(near, False)
+    near_copy(True).start()
+    near_copy(False).start()
+    forward(group_of(far - 3))
     id_wait(mate)
     compute(hi)
-    forward(group_of(far - 2))
 
     for c in range(chunks):
         pair_copy(hi, c).wait_recv()
     total = pair_keep[hi] + pair_recv[hi]
-    for k in range(far - 1):
-        g = group_of(far - 2 - k)
+    for same in (True, False):
+        near_copy(same).wait_recv()
+    total = total + (near_recv[0] + near_recv[1])
+    for k in range(far - 2):
+        g = group_of(far - 3 - k)
         for c in range(chunks):
             far_wait(g, c)
         total = total + far_recv[g]
@@ -267,10 +285,12 @@
     for j in range(1, n):
         id_copy((me + j) % n).wait_send()
     for c in range(chunks):
-        for g in range(far):
-            pair_copy(g, c).wait_send()
-        for j in range(1, far):
-            far_copy((hi + j) % far, c).wait_send()
+        pair_copy(hi, c).wait_send()
+        for k in range(far - 2):
+            pair_copy(group_of(k), c).wait_send()
+            far_copy(group_of(k), c).wait_send()
+    for same in (True, False):
+        near_copy(same).wait_send()
     for j in range(1, cols):
         gram_copy(j).wait_send()
 
@@ -308,6 +328,7 @@
             pltpu.VMEM(block, jnp.float32),
             pltpu.VMEM(block, jnp.float32),
             pltpu.VMEM(block, jnp.float32),
+            pltpu.VMEM((2,) + block[1:], jnp.float32),
             pltpu.VMEM((cols, pair_rows, here), jnp.float32),
             pltpu.VMEM((pair_rows, here), jnp.float32),
             pltpu.SemaphoreType.DMA((5,)),
@@ -317,6 +338,8 @@
             pltpu.SemaphoreType.DMA((far, chunks)),
             pltpu.SemaphoreType.DMA((far, chunks)),
             pltpu.SemaphoreType.DMA((far, chunks)),
+            pltpu.SemaphoreType.DMA((2,)),
+            pltpu.SemaphoreType.DMA((2,)),
             pltpu.SemaphoreType.DMA((cols,)),
             pltpu.SemaphoreType.DMA((cols,)),
         ],

time: 24.7 us -> 24.2 us (0.980)
  Pallas kernels: 22.6 us -> 22.2 us
    pallas_call x1, Pallas kernels: 22.6 us -> 22.2 us  [body(): pl.pallas_call(functools.partial(kernel, n, cols), out_shape=(pltpu.VMEM(...]
where the time goes in v4:
time: 24.2 us; the launch traced here: 24.1 us
  Pallas kernels  22.2 us (92%)
  local copies, waits for them, and re-layouts  1.23 us (5%)
  between operations  0.64 us (3%)
    pallas_call x1, Pallas kernels, body(): pl.pallas_call(functools.partial(kernel, n, cols), out_shape=(pltpu.VMEM(...  22.2 us
    unnamed x2, local copies, waits for them, and re-layouts  1.23 us

profile of v4, /device:TPU:0, one launch (start us, length us, event | category | flops | bytes accessed | tf_op | source)
XLA Modules:
  0.0 24.1 jit_solution(15082893923466095381)
XLA Ops:
  0.6 22.2 %shard_map.68 = (f32[32,4,128]{2,1,0:T(4,128)S(1)}, f32[10,32]{1,0:T(8,128)S(1)}) custom-call(f32[4,512,128]{2,1,0:T(8,128)} %tables_hbm.1, f32[32,128]{1,0:T(8,128)} %dense_hbm.1, s32[1,8,4,64]{3,2,1,0:T(4,128)} %rows_hbm.1, s32[1,8,4,64]{3,2,1,0:T(4,128)} %examples_hbm.1, s32[1,4,8]{2,1,0:T(4,128)} %bitcast.3), custom_call_target="tpu_custom_call" | custom-call | tf_op jit(solution)/shard_map/pallas_call | solution.py:309
  22.8 0.6 %copy.9 = f32[32,4,128]{2,1,0:T(4,128)} copy(f32[32,4,128]{2,1,0:T(4,128)S(1)} %get-tuple-element.6) | data formatting | bytes 131072
  23.5 0.6 %copy.10 = f32[32,10]{0,1:T(8,128)} copy(f32[32,10]{0,1:T(8,128)S(1)} %bitcast.2) | data formatting | bytes 2560
